TPU v7x, 32 devices: a whole 2x2x4 slice. The times are simulated.
32 devices in a mesh: dp: 2 (over x), lat: 4 (over y, core), lon: 4 (over z).
Axes of the slice: x: 2, y: 2, z: 4, core: 2. Of those that a mesh axis runs over, the one named last changes fastest.
Arguments:
- hidden_in: bfloat16 [2, 64, 512, 128], P('dp', 'lat', 'lon'), may hold values from -6 to 6
- conv_weight: bfloat16 [3, 3, 128, 128], replicated, may hold values from -0.1875 to 0.1875
- conv_bias: float32 [128], replicated, may hold values from -3 to 3
- proj_weight: float32 [128], replicated, may hold values from -5 to 5
- ocean_depth: float32 [64, 512], P('lat', 'lon'), may hold values from 0.5 to 2
- sea_mask: int32 [64, 512], P('lat', 'lon'), may hold values 0 or 1
- step_alpha: float32 [6], replicated, may hold values from 0.04 to 0.07
- step_beta: float32 [6], replicated, may hold values from 0.1 to 0.5
- surface_cotangent: float32 [2, 64, 512], P('dp', 'lat', 'lon'), may hold values from -20 to 20
Outputs:
- grad_hidden: bfloat16 [2, 64, 512, 128], P('dp', 'lat', 'lon')
- grad_weight: float32 [128, 3, 3, 128], P(('lat', 'lon'))
- grad_bias: float32 [128], replicated
- grad_proj: float32 [128], replicated
All inputs are finite; a program needn't handle non-finite values. No bound on the sum of `sea_mask` on one device may be relied on, other than what follows from the above.
Results may differ from a plain program's by a relative error of at most 0.01.
Values may be sent and summed in bfloat16 or wider, within the bound.
A program may use at most 64 MiB of HBM per device.

v0:
```python
import math
import jax
import jax.numpy as jnp
from jax import lax
from jax.sharding import PartitionSpec as P

ITERS = 6
helm_coef = 0.5


def extended(cells, sides, width, closed):
    for axis, dim in sides:
        count = lax.axis_size(axis)
        ends = count if closed else count - 1
        head = lax.slice_in_dim(cells, 0, width, axis=dim)
        tail = lax.slice_in_dim(cells, cells.shape[dim] - width, cells.shape[dim], axis=dim)
        cells = jnp.concatenate(
            [
                lax.ppermute(tail, axis, [(i, (i + 1) % count) for i in range(ends)]),
                cells,
                lax.ppermute(head, axis, [((i + 1) % count, i) for i in range(ends)]),
            ],
            axis=dim,
        )
    return cells


def operate(field_ext, mask_ext, depth_ext):
    rows_in = field_ext.shape[-2] - 2
    cols_in = field_ext.shape[-1] - 2
    center = field_ext[..., 1:-1, 1:-1]
    mask_mid = mask_ext[1:-1, 1:-1]
    depth_mid = depth_ext[1:-1, 1:-1]
    result = helm_coef * center
    for row_off, col_off in ((0, 1), (2, 1), (1, 0), (1, 2)):
        beside = field_ext[..., row_off : row_off + rows_in, col_off : col_off + cols_in]
        mask_near = mask_ext[row_off : row_off + rows_in, col_off : col_off + cols_in]
        depth_near = depth_ext[row_off : row_off + rows_in, col_off : col_off + cols_in]
        weight = mask_near * 0.5 * (depth_mid + depth_near)
        result = result + weight * (center - beside)
    return mask_mid * result


def solve_steps(adjoint_start, mask_ext, depth_ext, step_alpha, step_beta, widen):
    solution = jnp.zeros_like(adjoint_start)
    residual = adjoint_start
    direction = adjoint_start
    for turn_index in range(ITERS):
        solution = solution + step_alpha[turn_index] * direction
        if turn_index + 1 < ITERS:
            applied = operate(widen(direction), mask_ext, depth_ext)
            residual = residual - step_alpha[turn_index] * applied
            direction = residual + step_beta[turn_index] * direction
    return solution


def halo_field(field):
    field = extended(field, (("lat", 1),), 1, False)
    return extended(field, (("lon", 2),), 1, True)


def shards(
    hidden_in,
    conv_weight,
    conv_bias,
    proj_weight,
    ocean_depth,
    sea_mask,
    step_alpha,
    step_beta,
    surface_cotangent,
):
    samples, lat_rows, lon_cols, channels = hidden_in.shape
    mask_float = sea_mask.astype(jnp.float32)
    counted, summed = lax.psum(
        (jnp.sum(mask_float), jnp.sum(mask_float * surface_cotangent, axis=(1, 2))), ("lat", "lon")
    )
    adjoint_start = mask_float * (surface_cotangent - (summed / counted)[:, None, None])
    coefs = jnp.stack([mask_float, ocean_depth])
    coefs = extended(coefs, (("lat", 1),), 1, False)
    coefs = extended(coefs, (("lon", 2),), 1, True)
    solution = solve_steps(adjoint_start, coefs[0], coefs[1], step_alpha, step_beta, halo_field)
    forcing_grad = mask_float * solution
    padded = extended(hidden_in, (("lat", 1),), 1, False)
    padded = extended(padded, (("lon", 2),), 1, True)
    cell_count = samples * lat_rows * lon_cols
    shifted = [
        padded[:, row_off : row_off + lat_rows, col_off : col_off + lon_cols, :].reshape(
            cell_count, channels
        )
        for row_off in range(3)
        for col_off in range(3)
    ]
    preact = conv_bias
    for offset in range(9):
        preact = preact + jnp.dot(
            shifted[offset],
            conv_weight[offset // 3, offset % 3],
            preferred_element_type=jnp.float32,
        )
    sigma = jax.nn.sigmoid(preact)
    active = preact * sigma
    slope_act = sigma * (1.0 + preact * (1.0 - sigma))
    force_col = forcing_grad.reshape(cell_count)[:, None]
    grad_pre = (force_col * proj_weight * slope_act).astype(jnp.bfloat16)
    local_proj = jnp.sum(active * force_col, axis=0)
    local_bias = jnp.sum(grad_pre.astype(jnp.float32), axis=0)
    grad_ext = extended(
        grad_pre.reshape(samples, lat_rows, lon_cols, channels), (("lat", 1),), 1, False
    )
    grad_ext = extended(grad_ext, (("lon", 2),), 1, True)
    backed = jnp.zeros((cell_count, channels), jnp.float32)
    for row_off in range(3):
        for col_off in range(3):
            window = grad_ext[
                :, 2 - row_off : 2 - row_off + lat_rows, 2 - col_off : 2 - col_off + lon_cols, :
            ].reshape(cell_count, channels)
            backed = backed + lax.dot_general(
                window,
                conv_weight[row_off, col_off],
                (((1,), (1,)), ((), ())),
                preferred_element_type=jnp.float32,
            )
    grad_hidden = backed.reshape(samples, lat_rows, lon_cols, channels).astype(jnp.bfloat16)
    share = channels // lax.axis_size(("lat", "lon"))
    blocks = []
    for shifted_cols in shifted:
        blocks.append(
            lax.dot_general(
                shifted_cols, grad_pre, (((0,), (0,)), ((), ())), preferred_element_type=jnp.float32
            )
        )
    spatial = lax.psum_scatter(
        jnp.stack(blocks, axis=1).reshape(share * lax.axis_size(("lat", "lon")), 3, 3, channels),
        ("lat", "lon"),
        scatter_dimension=0,
        tiled=True,
    )
    own_weight = lax.psum(spatial, "dp")
    total_bias, total_proj = lax.psum((local_bias, local_proj), ("dp", "lat", "lon"))
    all_cells = cell_count * lax.axis_size("dp") * lax.axis_size("lat") * lax.axis_size("lon")
    grad_scale = 1.0 / math.sqrt(all_cells)
    return (grad_hidden, own_weight * grad_scale, total_bias * grad_scale, total_proj * grad_scale)


def solution(mesh):
    in_specs = (
        P("dp", "lat", "lon", None),
        P(),
        P(),
        P(),
        P("lat", "lon"),
        P("lat", "lon"),
        P(),
        P(),
        P("dp", "lat", "lon"),
    )
    out_specs = (P("dp", "lat", "lon", None), P(("lat", "lon"), None, None, None), P(), P())
    return jax.shard_map(shards, mesh=mesh, in_specs=in_specs, out_specs=out_specs, check_vma=False)
```

profile of v0, /device:TPU:0, one launch (start us, length us, event | category | flops | bytes accessed | tf_op | source)
XLA Modules:
  0.0 225.2 jit_solution(6670252528962750081)
XLA Ops:
  8.7 2.4 %collective-permute-start = (f32[2,1,128]{2,1,0:T(1,128)S(1)}, f32[2,1,128]{2,1,0:T(1,128)S(1)}, u32[]{:S(2)}, u32[]{:S(2)}) collective-permute-start(f32[2,1,128]{2,1,0:T(1,128)S(1)} %get-tuple-element.57), channel_id=1, source_target_pairs={{0,4},{4,8},{8,12},{1,5},{5,9},{9,13},{2,6},{6,10},{10,14},{3,7},{... | collective-permute-start | bytes 3080 | tf_op jit(solution)/shard_map/ppermute | solution.py:19
  15.0 36.6 %all-reduce.1 = (f32[1]{0:T(128)}, f32[1]{0:T(128)}) all-reduce(f32[1]{0:T(128)} %bitcast.2, f32[1]{0:T(128)} %bitcast.3), channel_id=1, replica_groups=mesh['dp'=2,'lat'=4,'lon'=4] {'lat','lon'}, use_global_device_ids=true, to_apply=%region_1.0 | all-reduce | flops 2 | bytes 16 | tf_op jit(solution)/shard_map/psum | solution.py:75
  56.2 1.5 fusion.171
  57.8 1.5 fusion.172
  61.0 3.7 %collective-permute-start.3 = (f32[2,18,1]{2,1,0:T(8,128)S(1)}, f32[2,18,1]{2,1,0:T(8,128)S(1)}, u32[]{:S(2)}, u32[]{:S(2)}) collective-permute-start(f32[2,18,1]{2,1,0:T(8,128)S(1)} %get-tuple-element.56), channel_id=1, source_target_pairs={{1,0},{2,1},{3,2},{0,3},{5,4},{6,5},{7,6},{4,7},{9,8},{10,9},{11,1... | collective-permute-start | bytes 440 | tf_op jit(solution)/shard_map/ppermute | solution.py:21
  64.7 2.0 collective-permute-start.7
  69.7 2.6 %collective-permute-start.8 = (f32[1,1,128]{2,1,0:T(1,128)S(1)}, f32[1,1,128]{2,1,0:T(1,128)S(1)}, u32[]{:S(2)}, u32[]{:S(2)}) collective-permute-start(f32[1,1,128]{2,1,0:T(1,128)S(1)} %get-tuple-element.75), channel_id=1, source_target_pairs={{0,4},{4,8},{8,12},{1,5},{5,9},{9,13},{2,6},{6,10},{10,14},{3,7},{... | collective-permute-start | bytes 1544 | tf_op jit(solution)/shard_map/ppermute | solution.py:19
  73.6 4.7 %collective-permute-done.9 = f32[1,1,128]{2,1,0:T(1,128)S(1)} collective-permute-done((f32[1,1,128]{2,1,0:T(1,128)S(1)}, f32[1,1,128]{2,1,0:T(1,128)S(1)}, u32[]{:S(2)}, u32[]{:S(2)}) %collective-permute-start.9) | collective-permute-done | bytes 544 | tf_op jit(solution)/shard_map/ppermute | solution.py:21
  78.4 3.8 %collective-permute-start.11 = (f32[1,18,1]{2,1,0:T(8,128)S(1)}, f32[1,18,1]{2,1,0:T(8,128)S(1)}, u32[]{:S(2)}, u32[]{:S(2)}) collective-permute-start(f32[1,18,1]{2,1,0:T(8,128)S(1)} %get-tuple-element.66), channel_id=1, source_target_pairs={{1,0},{2,1},{3,2},{0,3},{5,4},{6,5},{7,6},{4,7},{9,8},{10,9},{11,1... | collective-permute-start | bytes 224 | tf_op jit(solution)/shard_map/ppermute | solution.py:21
  82.2 1.7 collective-permute-done.10
  83.9 1.3 multiply_add_fusion.2
  85.2 3.3 %collective-permute-start.12 = (f32[1,1,128]{2,1,0:T(1,128)S(1)}, f32[1,1,128]{2,1,0:T(1,128)S(1)}, u32[]{:S(2)}, u32[]{:S(2)}) collective-permute-start(f32[1,1,128]{2,1,0:T(1,128)S(1)} %get-tuple-element.73), channel_id=1, source_target_pairs={{0,4},{4,8},{8,12},{1,5},{5,9},{9,13},{2,6},{6,10},{10,14},{3,7},{... | collective-permute-start | bytes 1544 | tf_op jit(solution)/shard_map/ppermute | solution.py:19
  89.9 2.2 collective-permute-done.13
  93.3 2.8 %collective-permute-start.15 = (f32[1,18,1]{2,1,0:T(8,128)S(1)}, f32[1,18,1]{2,1,0:T(8,128)S(1)}, u32[]{:S(2)}, u32[]{:S(2)}) collective-permute-start(f32[1,18,1]{2,1,0:T(8,128)S(1)} %get-tuple-element.64), channel_id=1, source_target_pairs={{1,0},{2,1},{3,2},{0,3},{5,4},{6,5},{7,6},{4,7},{9,8},{10,9},{11,1... | collective-permute-start | bytes 224 | tf_op jit(solution)/shard_map/ppermute | solution.py:21
  96.1 1.6 collective-permute-done.14
  97.7 1.4 multiply_add_fusion.1
  99.0 3.4 %collective-permute-start.16 = (f32[1,1,128]{2,1,0:T(1,128)S(1)}, f32[1,1,128]{2,1,0:T(1,128)S(1)}, u32[]{:S(2)}, u32[]{:S(2)}) collective-permute-start(f32[1,1,128]{2,1,0:T(1,128)S(1)} %get-tuple-element.71), channel_id=1, source_target_pairs={{0,4},{4,8},{8,12},{1,5},{5,9},{9,13},{2,6},{6,10},{10,14},{3,7},{... | collective-permute-start | bytes 1544 | tf_op jit(solution)/shard_map/ppermute | solution.py:19
  103.7 2.2 collective-permute-done.17
  107.3 2.6 %collective-permute-start.19 = (f32[1,18,1]{2,1,0:T(8,128)S(1)}, f32[1,18,1]{2,1,0:T(8,128)S(1)}, u32[]{:S(2)}, u32[]{:S(2)}) collective-permute-start(f32[1,18,1]{2,1,0:T(8,128)S(1)} %get-tuple-element.62), channel_id=1, source_target_pairs={{1,0},{2,1},{3,2},{0,3},{5,4},{6,5},{7,6},{4,7},{9,8},{10,9},{11,1... | collective-permute-start | bytes 224 | tf_op jit(solution)/shard_map/ppermute | solution.py:21
  109.9 1.6 collective-permute-done.18
  112.8 3.4 %collective-permute-start.20 = (f32[1,1,128]{2,1,0:T(1,128)S(1)}, f32[1,1,128]{2,1,0:T(1,128)S(1)}, u32[]{:S(2)}, u32[]{:S(2)}) collective-permute-start(f32[1,1,128]{2,1,0:T(1,128)S(1)} %get-tuple-element.69), channel_id=1, source_target_pairs={{0,4},{4,8},{8,12},{1,5},{5,9},{9,13},{2,6},{6,10},{10,14},{3,7},{... | collective-permute-start | bytes 1544 | tf_op jit(solution)/shard_map/ppermute | solution.py:19
  117.5 3.5 %collective-permute-start.24 = (bf16[1,1,128,128]{3,2,1,0:T(8,128)(2,1)S(1)}, bf16[1,1,128,128]{3,2,1,0:T(8,128)(2,1)S(1)}, u32[]{:S(2)}, u32[]{:S(2)}) collective-permute-start(bf16[1,1,128,128]{3,2,1,0:T(8,128)(2,1)S(1)} %get-tuple-element.52), channel_id=1, source_target_pairs={{0,4},{4,8},{8,12},{1,5},{5,9},{9,13},{2,6},{6,10},{10,14},{3,7},{... | collective-permute-start | bytes 98312 | tf_op jit(solution)/shard_map/ppermute | solution.py:19
  123.7 2.6 %collective-permute-start.23 = (f32[1,18,1]{2,1,0:T(8,128)S(1)}, f32[1,18,1]{2,1,0:T(8,128)S(1)}, u32[]{:S(2)}, u32[]{:S(2)}) collective-permute-start(f32[1,18,1]{2,1,0:T(8,128)S(1)} %get-tuple-element.60), channel_id=1, source_target_pairs={{1,0},{2,1},{3,2},{0,3},{5,4},{6,5},{7,6},{4,7},{9,8},{10,9},{11,1... | collective-permute-start | bytes 224 | tf_op jit(solution)/shard_map/ppermute | solution.py:21
  126.3 1.6 collective-permute-done.22
  128.0 4.5 %fusion.69 = f32[2048]{0:T(1024)S(1)} fusion(f32[1,16,128]{2,1,0:T(8,128)S(1)} %get-tuple-element.11, f32[1,16,128]{2,1,0:T(8,128)S(1)} %get-tuple-element.21, f32[1,16,128]{2,1,0:T(8,128)S(1)} %get-tuple-element.10, f32[1,18,1]{2,1,0:T(8,128)S(1)} %collective-permute-done.23, f32[1,1,128]{2,1,0:T(1,128)S(1)} %collective-permute-done.21, ...), kind=kLoop, calls=%fused_computation.128 | loop fusion | flops 79872 | bytes 107692 | tf_op jit(solution)/shard_map/mul | solution.py:105
  132.9 1.4 collective-permute-start.26
  134.2 2.6 %collective-permute-start.27 = (bf16[1,18,1,128]{3,2,1,0:T(2,128)(2,1)S(1)}, bf16[1,18,1,128]{3,2,1,0:T(2,128)(2,1)S(1)}, u32[]{:S(2)}, u32[]{:S(2)}) collective-permute-start(bf16[1,18,1,128]{3,2,1,0:T(2,128)(2,1)S(1)} %get-tuple-element.43), channel_id=1, source_target_pairs={{1,0},{2,1},{3,2},{0,3},{5,4},{6,5},{7,6},{4,7},{9,8},{10,9},{11,1... | collective-permute-start | bytes 13832 | tf_op jit(solution)/shard_map/ppermute | solution.py:21
  146.9 2.2 collective-permute-start.28
  150.4 45.0 %all-reduce = (f32[128]{0:T(128)S(1)}, f32[128]{0:T(128)S(1)}) all-reduce(f32[128]{0:T(128)S(1)} %get-tuple-element.8, f32[128]{0:T(128)S(1)} %get-tuple-element.22), channel_id=1, replica_groups=mesh['dp'=2,'lat'=4,'lon'=4] {'dp','lat','lon'}, use_global_device_ids=true, to_apply=%region_7.0 | all-reduce | flops 256 | bytes 2048 | tf_op jit(solution)/shard_map/psum | solution.py:140
  196.0 2.4 %collective-permute-start.30 = (bf16[1,18,1,128]{3,2,1,0:T(2,128)(2,1)S(1)}, bf16[1,18,1,128]{3,2,1,0:T(2,128)(2,1)S(1)}, u32[]{:S(2)}, u32[]{:S(2)}) collective-permute-start(bf16[1,18,1,128]{3,2,1,0:T(2,128)(2,1)S(1)} %get-tuple-element.37), channel_id=1, source_target_pairs={{1,0},{2,1},{3,2},{0,3},{5,4},{6,5},{7,6},{4,7},{9,8},{10,9},{11,1... | collective-permute-start | bytes 13832 | tf_op jit(solution)/shard_map/ppermute | solution.py:21
  199.7 4.1 %collective-permute-done.31 = bf16[1,18,1,128]{3,2,1,0:T(2,128)(2,1)S(1)} collective-permute-done((bf16[1,18,1,128]{3,2,1,0:T(2,128)(2,1)S(1)}, bf16[1,18,1,128]{3,2,1,0:T(2,128)(2,1)S(1)}, u32[]{:S(2)}, u32[]{:S(2)}) %collective-permute-start.31) | collective-permute-done | bytes 4640 | tf_op jit(solution)/shard_map/ppermute | solution.py:19
  207.9 9.9 %psum.37 = f32[8,3,3,128]{3,0,2,1:T(8,128)S(1)} all-reduce(f32[8,3,3,128]{3,0,2,1:T(8,128)} %reduce-scatter.2.cloned.1.call-done), channel_id=1, replica_groups=mesh['dp'=2,'lat'=4,'lon'=4] {'dp'}, use_global_device_ids=true, to_apply=%region_5.0 | all-reduce | flops 9216 | bytes 73728 | tf_op jit(solution)/shard_map/psum | solution.py:139
  (121 shorter events, 43.4 us)
Async XLA Ops:
  7.2 200.7 %reduce-scatter.2.cloned.1.call-start = ((), (), s32[]{:S(2)}) async-start(), calls=%async_computation.1 | async-start | bytes 626688 | tf_op jit(solution)/shard_map/reduce_scatter | solution.py:133
  8.7 51.3 %collective-permute-start = (f32[2,1,128]{2,1,0:T(1,128)S(1)}, f32[2,1,128]{2,1,0:T(1,128)S(1)}, u32[]{:S(2)}, u32[]{:S(2)}) collective-permute-start(f32[2,1,128]{2,1,0:T(1,128)S(1)} %get-tuple-element.57), channel_id=1, source_target_pairs={{0,4},{4,8},{8,12},{1,5},{5,9},{9,13},{2,6},{6,10},{10,14},{3,7},{... | collective-permute-start | bytes 3080 | tf_op jit(solution)/shard_map/ppermute | solution.py:19
  11.1 49.0 %collective-permute-start.1 = (f32[2,1,128]{2,1,0:T(1,128)S(1)}, f32[2,1,128]{2,1,0:T(1,128)S(1)}, u32[]{:S(2)}, u32[]{:S(2)}) collective-permute-start(f32[2,1,128]{2,1,0:T(1,128)S(1)} %get-tuple-element.58), channel_id=1, source_target_pairs={{4,0},{8,4},{12,8},{5,1},{9,5},{13,9},{6,2},{10,6},{14,10},{7,3},{... | collective-permute-start | bytes 3080 | tf_op jit(solution)/shard_map/ppermute | solution.py:21
  53.6 5.6 %collective-permute-start.4 = (f32[1,1,128]{2,1,0:T(1,128)S(1)}, f32[1,1,128]{2,1,0:T(1,128)S(1)}, u32[]{:S(2)}, u32[]{:S(2)}) collective-permute-start(f32[1,1,128]{2,1,0:T(1,128)S(1)} %get-tuple-element.77), channel_id=1, source_target_pairs={{0,4},{4,8},{8,12},{1,5},{5,9},{9,13},{2,6},{6,10},{10,14},{3,7},{... | collective-permute-start | bytes 1544 | tf_op jit(solution)/shard_map/ppermute | solution.py:19
  54.9 5.0 %collective-permute-start.5 = (f32[1,1,128]{2,1,0:T(1,128)S(1)}, f32[1,1,128]{2,1,0:T(1,128)S(1)}, u32[]{:S(2)}, u32[]{:S(2)}) collective-permute-start(f32[1,1,128]{2,1,0:T(1,128)S(1)} %get-tuple-element.78), channel_id=1, source_target_pairs={{4,0},{8,4},{12,8},{5,1},{9,5},{13,9},{6,2},{10,6},{14,10},{7,3},{... | collective-permute-start | bytes 1544 | tf_op jit(solution)/shard_map/ppermute | solution.py:21
  60.0 7.5 %collective-permute-start.6 = (f32[1,18,1]{2,1,0:T(8,128)S(1)}, f32[1,18,1]{2,1,0:T(8,128)S(1)}, u32[]{:S(2)}, u32[]{:S(2)}) collective-permute-start(f32[1,18,1]{2,1,0:T(8,128)S(1)} %get-tuple-element.67), channel_id=1, source_target_pairs={{0,1},{1,2},{2,3},{3,0},{4,5},{5,6},{6,7},{7,4},{8,9},{9,10},{10,1... | collective-permute-start | bytes 224 | tf_op jit(solution)/shard_map/ppermute | solution.py:19
  60.8 5.8 %collective-permute-start.2 = (f32[2,18,1]{2,1,0:T(8,128)S(1)}, f32[2,18,1]{2,1,0:T(8,128)S(1)}, u32[]{:S(2)}, u32[]{:S(2)}) collective-permute-start(f32[2,18,1]{2,1,0:T(8,128)S(1)} %get-tuple-element.55), channel_id=1, source_target_pairs={{0,1},{1,2},{2,3},{3,0},{4,5},{5,6},{6,7},{7,4},{8,9},{9,10},{10,1... | collective-permute-start | bytes 440 | tf_op jit(solution)/shard_map/ppermute | solution.py:19
  61.0 5.7 %collective-permute-start.3 = (f32[2,18,1]{2,1,0:T(8,128)S(1)}, f32[2,18,1]{2,1,0:T(8,128)S(1)}, u32[]{:S(2)}, u32[]{:S(2)}) collective-permute-start(f32[2,18,1]{2,1,0:T(8,128)S(1)} %get-tuple-element.56), channel_id=1, source_target_pairs={{1,0},{2,1},{3,2},{0,3},{5,4},{6,5},{7,6},{4,7},{9,8},{10,9},{11,1... | collective-permute-start | bytes 440 | tf_op jit(solution)/shard_map/ppermute | solution.py:21
  64.7 3.7 %collective-permute-start.7 = (f32[1,18,1]{2,1,0:T(8,128)S(1)}, f32[1,18,1]{2,1,0:T(8,128)S(1)}, u32[]{:S(2)}, u32[]{:S(2)}) collective-permute-start(f32[1,18,1]{2,1,0:T(8,128)S(1)} %get-tuple-element.68), channel_id=1, source_target_pairs={{1,0},{2,1},{3,2},{0,3},{5,4},{6,5},{7,6},{4,7},{9,8},{10,9},{11,1... | collective-permute-start | bytes 224 | tf_op jit(solution)/shard_map/ppermute | solution.py:21
  69.7 3.9 %collective-permute-start.8 = (f32[1,1,128]{2,1,0:T(1,128)S(1)}, f32[1,1,128]{2,1,0:T(1,128)S(1)}, u32[]{:S(2)}, u32[]{:S(2)}) collective-permute-start(f32[1,1,128]{2,1,0:T(1,128)S(1)} %get-tuple-element.75), channel_id=1, source_target_pairs={{0,4},{4,8},{8,12},{1,5},{5,9},{9,13},{2,6},{6,10},{10,14},{3,7},{... | collective-permute-start | bytes 1544 | tf_op jit(solution)/shard_map/ppermute | solution.py:19
  72.3 6.0 %collective-permute-start.9 = (f32[1,1,128]{2,1,0:T(1,128)S(1)}, f32[1,1,128]{2,1,0:T(1,128)S(1)}, u32[]{:S(2)}, u32[]{:S(2)}) collective-permute-start(f32[1,1,128]{2,1,0:T(1,128)S(1)} %get-tuple-element.76), channel_id=1, source_target_pairs={{4,0},{8,4},{12,8},{5,1},{9,5},{13,9},{6,2},{10,6},{14,10},{7,3},{... | collective-permute-start | bytes 1544 | tf_op jit(solution)/shard_map/ppermute | solution.py:21
  78.4 5.5 %collective-permute-start.10 = (f32[1,18,1]{2,1,0:T(8,128)S(1)}, f32[1,18,1]{2,1,0:T(8,128)S(1)}, u32[]{:S(2)}, u32[]{:S(2)}) collective-permute-start(f32[1,18,1]{2,1,0:T(8,128)S(1)} %get-tuple-element.65), channel_id=1, source_target_pairs={{0,1},{1,2},{2,3},{3,0},{4,5},{5,6},{6,7},{7,4},{8,9},{9,10},{10,1... | collective-permute-start | bytes 224 | tf_op jit(solution)/shard_map/ppermute | solution.py:19
  78.4 5.5 %collective-permute-start.11 = (f32[1,18,1]{2,1,0:T(8,128)S(1)}, f32[1,18,1]{2,1,0:T(8,128)S(1)}, u32[]{:S(2)}, u32[]{:S(2)}) collective-permute-start(f32[1,18,1]{2,1,0:T(8,128)S(1)} %get-tuple-element.66), channel_id=1, source_target_pairs={{1,0},{2,1},{3,2},{0,3},{5,4},{6,5},{7,6},{4,7},{9,8},{10,9},{11,1... | collective-permute-start | bytes 224 | tf_op jit(solution)/shard_map/ppermute | solution.py:21
  85.2 4.6 %collective-permute-start.12 = (f32[1,1,128]{2,1,0:T(1,128)S(1)}, f32[1,1,128]{2,1,0:T(1,128)S(1)}, u32[]{:S(2)}, u32[]{:S(2)}) collective-permute-start(f32[1,1,128]{2,1,0:T(1,128)S(1)} %get-tuple-element.73), channel_id=1, source_target_pairs={{0,4},{4,8},{8,12},{1,5},{5,9},{9,13},{2,6},{6,10},{10,14},{3,7},{... | collective-permute-start | bytes 1544 | tf_op jit(solution)/shard_map/ppermute | solution.py:19
  88.6 3.5 %collective-permute-start.13 = (f32[1,1,128]{2,1,0:T(1,128)S(1)}, f32[1,1,128]{2,1,0:T(1,128)S(1)}, u32[]{:S(2)}, u32[]{:S(2)}) collective-permute-start(f32[1,1,128]{2,1,0:T(1,128)S(1)} %get-tuple-element.74), channel_id=1, source_target_pairs={{4,0},{8,4},{12,8},{5,1},{9,5},{13,9},{6,2},{10,6},{14,10},{7,3},{... | collective-permute-start | bytes 1544 | tf_op jit(solution)/shard_map/ppermute | solution.py:21
  92.2 5.5 %collective-permute-start.14 = (f32[1,18,1]{2,1,0:T(8,128)S(1)}, f32[1,18,1]{2,1,0:T(8,128)S(1)}, u32[]{:S(2)}, u32[]{:S(2)}) collective-permute-start(f32[1,18,1]{2,1,0:T(8,128)S(1)} %get-tuple-element.63), channel_id=1, source_target_pairs={{0,1},{1,2},{2,3},{3,0},{4,5},{5,6},{6,7},{7,4},{8,9},{9,10},{10,1... | collective-permute-start | bytes 224 | tf_op jit(solution)/shard_map/ppermute | solution.py:19
  93.3 4.4 %collective-permute-start.15 = (f32[1,18,1]{2,1,0:T(8,128)S(1)}, f32[1,18,1]{2,1,0:T(8,128)S(1)}, u32[]{:S(2)}, u32[]{:S(2)}) collective-permute-start(f32[1,18,1]{2,1,0:T(8,128)S(1)} %get-tuple-element.64), channel_id=1, source_target_pairs={{1,0},{2,1},{3,2},{0,3},{5,4},{6,5},{7,6},{4,7},{9,8},{10,9},{11,1... | collective-permute-start | bytes 224 | tf_op jit(solution)/shard_map/ppermute | solution.py:21
  99.0 4.7 %collective-permute-start.16 = (f32[1,1,128]{2,1,0:T(1,128)S(1)}, f32[1,1,128]{2,1,0:T(1,128)S(1)}, u32[]{:S(2)}, u32[]{:S(2)}) collective-permute-start(f32[1,1,128]{2,1,0:T(1,128)S(1)} %get-tuple-element.71), channel_id=1, source_target_pairs={{0,4},{4,8},{8,12},{1,5},{5,9},{9,13},{2,6},{6,10},{10,14},{3,7},{... | collective-permute-start | bytes 1544 | tf_op jit(solution)/shard_map/ppermute | solution.py:19
  106.0 5.5 %collective-permute-start.18 = (f32[1,18,1]{2,1,0:T(8,128)S(1)}, f32[1,18,1]{2,1,0:T(8,128)S(1)}, u32[]{:S(2)}, u32[]{:S(2)}) collective-permute-start(f32[1,18,1]{2,1,0:T(8,128)S(1)} %get-tuple-element.61), channel_id=1, source_target_pairs={{0,1},{1,2},{2,3},{3,0},{4,5},{5,6},{6,7},{7,4},{8,9},{9,10},{10,1... | collective-permute-start | bytes 224 | tf_op jit(solution)/shard_map/ppermute | solution.py:19
  107.3 4.2 %collective-permute-start.19 = (f32[1,18,1]{2,1,0:T(8,128)S(1)}, f32[1,18,1]{2,1,0:T(8,128)S(1)}, u32[]{:S(2)}, u32[]{:S(2)}) collective-permute-start(f32[1,18,1]{2,1,0:T(8,128)S(1)} %get-tuple-element.62), channel_id=1, source_target_pairs={{1,0},{2,1},{3,2},{0,3},{5,4},{6,5},{7,6},{4,7},{9,8},{10,9},{11,1... | collective-permute-start | bytes 224 | tf_op jit(solution)/shard_map/ppermute | solution.py:21
  112.8 9.5 %collective-permute-start.20 = (f32[1,1,128]{2,1,0:T(1,128)S(1)}, f32[1,1,128]{2,1,0:T(1,128)S(1)}, u32[]{:S(2)}, u32[]{:S(2)}) collective-permute-start(f32[1,1,128]{2,1,0:T(1,128)S(1)} %get-tuple-element.69), channel_id=1, source_target_pairs={{0,4},{4,8},{8,12},{1,5},{5,9},{9,13},{2,6},{6,10},{10,14},{3,7},{... | collective-permute-start | bytes 1544 | tf_op jit(solution)/shard_map/ppermute | solution.py:19
  116.2 6.1 %collective-permute-start.21 = (f32[1,1,128]{2,1,0:T(1,128)S(1)}, f32[1,1,128]{2,1,0:T(1,128)S(1)}, u32[]{:S(2)}, u32[]{:S(2)}) collective-permute-start(f32[1,1,128]{2,1,0:T(1,128)S(1)} %get-tuple-element.70), channel_id=1, source_target_pairs={{4,0},{8,4},{12,8},{5,1},{9,5},{13,9},{6,2},{10,6},{14,10},{7,3},{... | collective-permute-start | bytes 1544 | tf_op jit(solution)/shard_map/ppermute | solution.py:21
  117.5 14.9 %collective-permute-start.24 = (bf16[1,1,128,128]{3,2,1,0:T(8,128)(2,1)S(1)}, bf16[1,1,128,128]{3,2,1,0:T(8,128)(2,1)S(1)}, u32[]{:S(2)}, u32[]{:S(2)}) collective-permute-start(bf16[1,1,128,128]{3,2,1,0:T(8,128)(2,1)S(1)} %get-tuple-element.52), channel_id=1, source_target_pairs={{0,4},{4,8},{8,12},{1,5},{5,9},{9,13},{2,6},{6,10},{10,14},{3,7},{... | collective-permute-start | bytes 98312 | tf_op jit(solution)/shard_map/ppermute | solution.py:19
  121.0 11.5 %collective-permute-start.25 = (bf16[1,1,128,128]{3,2,1,0:T(8,128)(2,1)S(1)}, bf16[1,1,128,128]{3,2,1,0:T(8,128)(2,1)S(1)}, u32[]{:S(2)}, u32[]{:S(2)}) collective-permute-start(bf16[1,1,128,128]{3,2,1,0:T(8,128)(2,1)S(1)} %get-tuple-element.51), channel_id=1, source_target_pairs={{4,0},{8,4},{12,8},{5,1},{9,5},{13,9},{6,2},{10,6},{14,10},{7,3},{... | collective-permute-start | bytes 98312 | tf_op jit(solution)/shard_map/ppermute | solution.py:21
  122.4 5.5 %collective-permute-start.22 = (f32[1,18,1]{2,1,0:T(8,128)S(1)}, f32[1,18,1]{2,1,0:T(8,128)S(1)}, u32[]{:S(2)}, u32[]{:S(2)}) collective-permute-start(f32[1,18,1]{2,1,0:T(8,128)S(1)} %get-tuple-element.59), channel_id=1, source_target_pairs={{0,1},{1,2},{2,3},{3,0},{4,5},{5,6},{6,7},{7,4},{8,9},{9,10},{10,1... | collective-permute-start | bytes 224 | tf_op jit(solution)/shard_map/ppermute | solution.py:19
  123.7 4.2 %collective-permute-start.23 = (f32[1,18,1]{2,1,0:T(8,128)S(1)}, f32[1,18,1]{2,1,0:T(8,128)S(1)}, u32[]{:S(2)}, u32[]{:S(2)}) collective-permute-start(f32[1,18,1]{2,1,0:T(8,128)S(1)} %get-tuple-element.60), channel_id=1, source_target_pairs={{1,0},{2,1},{3,2},{0,3},{5,4},{6,5},{7,6},{4,7},{9,8},{10,9},{11,1... | collective-permute-start | bytes 224 | tf_op jit(solution)/shard_map/ppermute | solution.py:21
  132.9 5.6 %collective-permute-start.26 = (bf16[1,18,1,128]{3,2,1,0:T(2,128)(2,1)S(1)}, bf16[1,18,1,128]{3,2,1,0:T(2,128)(2,1)S(1)}, u32[]{:S(2)}, u32[]{:S(2)}) collective-permute-start(bf16[1,18,1,128]{3,2,1,0:T(2,128)(2,1)S(1)} %get-tuple-element.42), channel_id=1, source_target_pairs={{0,1},{1,2},{2,3},{3,0},{4,5},{5,6},{6,7},{7,4},{8,9},{9,10},{10,1... | collective-permute-start | bytes 13832 | tf_op jit(solution)/shard_map/ppermute | solution.py:19
  134.2 4.2 %collective-permute-start.27 = (bf16[1,18,1,128]{3,2,1,0:T(2,128)(2,1)S(1)}, bf16[1,18,1,128]{3,2,1,0:T(2,128)(2,1)S(1)}, u32[]{:S(2)}, u32[]{:S(2)}) collective-permute-start(bf16[1,18,1,128]{3,2,1,0:T(2,128)(2,1)S(1)} %get-tuple-element.43), channel_id=1, source_target_pairs={{1,0},{2,1},{3,2},{0,3},{5,4},{6,5},{7,6},{4,7},{9,8},{10,9},{11,1... | collective-permute-start | bytes 13832 | tf_op jit(solution)/shard_map/ppermute | solution.py:21
  146.9 49.1 %collective-permute-start.28 = (bf16[1,1,128,128]{3,2,1,0:T(8,128)(2,1)S(1)}, bf16[1,1,128,128]{3,2,1,0:T(8,128)(2,1)S(1)}, u32[]{:S(2)}, u32[]{:S(2)}) collective-permute-start(bf16[1,1,128,128]{3,2,1,0:T(8,128)(2,1)S(1)} %get-tuple-element.46), channel_id=1, source_target_pairs={{0,4},{4,8},{8,12},{1,5},{5,9},{9,13},{2,6},{6,10},{10,14},{3,7},{... | collective-permute-start | bytes 98312 | tf_op jit(solution)/shard_map/ppermute | solution.py:19
  149.1 46.9 %collective-permute-start.29 = (bf16[1,1,128,128]{3,2,1,0:T(8,128)(2,1)S(1)}, bf16[1,1,128,128]{3,2,1,0:T(8,128)(2,1)S(1)}, u32[]{:S(2)}, u32[]{:S(2)}) collective-permute-start(bf16[1,1,128,128]{3,2,1,0:T(8,128)(2,1)S(1)} %get-tuple-element.47), channel_id=1, source_target_pairs={{4,0},{8,4},{12,8},{5,1},{9,5},{13,9},{6,2},{10,6},{14,10},{7,3},{... | collective-permute-start | bytes 98312 | tf_op jit(solution)/shard_map/ppermute | solution.py:21
  196.0 3.7 %collective-permute-start.30 = (bf16[1,18,1,128]{3,2,1,0:T(2,128)(2,1)S(1)}, bf16[1,18,1,128]{3,2,1,0:T(2,128)(2,1)S(1)}, u32[]{:S(2)}, u32[]{:S(2)}) collective-permute-start(bf16[1,18,1,128]{3,2,1,0:T(2,128)(2,1)S(1)} %get-tuple-element.37), channel_id=1, source_target_pairs={{1,0},{2,1},{3,2},{0,3},{5,4},{6,5},{7,6},{4,7},{9,8},{10,9},{11,1... | collective-permute-start | bytes 13832 | tf_op jit(solution)/shard_map/ppermute | solution.py:21
  198.3 5.5 %collective-permute-start.31 = (bf16[1,18,1,128]{3,2,1,0:T(2,128)(2,1)S(1)}, bf16[1,18,1,128]{3,2,1,0:T(2,128)(2,1)S(1)}, u32[]{:S(2)}, u32[]{:S(2)}) collective-permute-start(bf16[1,18,1,128]{3,2,1,0:T(2,128)(2,1)S(1)} %get-tuple-element.38), channel_id=1, source_target_pairs={{0,1},{1,2},{2,3},{3,0},{4,5},{5,6},{6,7},{7,4},{8,9},{9,10},{10,1... | collective-permute-start | bytes 13832 | tf_op jit(solution)/shard_map/ppermute | solution.py:19
  (7 other events, 241.2 us)
Sparse Core Ops, SparseCore 0:
  147.0 57.9 reduce-scatter.1
where the time goes:
time: 227 us; the launch traced here: 225 us
  blocking collectives  91.5 us (40%)
  starting transfers between devices  60.1 us (26%)
  waiting for transfers between devices  23.7 us (10%)
  other arithmetic  18.9 us (8%)
  between operations  15.9 us (7%)
  matrix products  9.55 us (4%)
  local copies, waits for them, and re-layouts  5.66 us (2%)
    psum x1, blocking collectives, shards(): lax.psum((local_bias, local_proj), ('dp', 'lat', 'lon'))  45 us
    psum x1, blocking collectives, shards(): lax.psum((jnp.sum(mask_float), jnp.sum(mask_float * surface_cotangent, ax...  36.6 us
    ppermute x16, starting transfers between devices, extended(): lax.ppermute(head, axis, [((i + 1) % count, i) for i in range(ends)])  32.9 us
    ppermute x16, starting transfers between devices, extended(): lax.ppermute(tail, axis, [(i, (i + 1) % count) for i in range(ends)])  27.1 us
    ppermute x16, waiting for transfers between devices, extended(): lax.ppermute(tail, axis, [(i, (i + 1) % count) for i in range(ends)])  11.9 us
    ppermute x16, waiting for transfers between devices, extended(): lax.ppermute(head, axis, [((i + 1) % count, i) for i in range(ends)])  11.7 us
    psum x1, blocking collectives, shards(): own_weight = lax.psum(spatial, 'dp')  9.87 us
    add x4, other arithmetic, solve_steps(): direction = residual + step_beta[turn_index] * direction  5.32 us
  transfers between devices with their start and end apart: 33, of which 12 were waited for; matrix products, arithmetic and copies ran while one was open for 8% of the time, Pallas kernels for 0%

commit v1 on v0

--- a/solution.py
+++ b/solution.py
@@ -6,6 +6,11 @@
 
 ITERS = 6
 helm_coef = 0.5
+
+
+def axis_by_axis(x, inner_axis, outer_axis):
+    partial = lax.psum(x, inner_axis)
+    return lax.psum(partial, outer_axis)
 
 
 def extended(cells, sides, width, closed):
@@ -137,7 +142,7 @@
         tiled=True,
     )
     own_weight = lax.psum(spatial, "dp")
-    total_bias, total_proj = lax.psum((local_bias, local_proj), ("dp", "lat", "lon"))
+    total_bias, total_proj = axis_by_axis((local_bias, local_proj), "dp", ("lat", "lon"))
     all_cells = cell_count * lax.axis_size("dp") * lax.axis_size("lat") * lax.axis_size("lon")
     grad_scale = 1.0 / math.sqrt(all_cells)
     return (grad_hidden, own_weight * grad_scale, total_bias * grad_scale, total_proj * grad_scale)

time: 227 us -> 260 us (1.15)
  waiting for transfers between devices: 23.7 us -> 70.4 us
  blocking collectives: 91.5 us -> 76.7 us
    reduce_scatter x1, waiting for transfers between devices: 0.01 us -> 42.9 us  [shards(): lax.psum_scatter(jnp.stack(blocks, axis=1).reshape(share * lax.axis_size(...]
    psum x1, blocking collectives: 45 us -> 31.1 us  [axis_by_axis(): return lax.psum(partial, outer_axis)]
    ppermute x16, waiting for transfers between devices: 11.7 us -> 15.6 us  [extended(): lax.ppermute(head, axis, [((i + 1) % count, i) for i in range(ends)])]
  transfers between devices with their start and end apart: 33 -> 33, of which waited for: 12 -> 14; matrix products, arithmetic and copies ran while one was open for 8% -> 7% of each run, Pallas kernels for 0% -> 0%
where the time goes in v1:
time: 260 us; the launch traced here: 259 us
  blocking collectives  76.7 us (30%)
  waiting for transfers between devices  70.4 us (27%)
  starting transfers between devices  61.7 us (24%)
  other arithmetic  19 us (7%)
  between operations  15.9 us (6%)
  matrix products  9.55 us (4%)
  local copies, waits for them, and re-layouts  5.76 us (2%)
    reduce_scatter x1, waiting for transfers between devices, shards(): lax.psum_scatter(jnp.stack(blocks, axis=1).reshape(share * lax.axis_size(...  42.9 us
    psum x1, blocking collectives, shards(): lax.psum((jnp.sum(mask_float), jnp.sum(mask_float * surface_cotangent, ax...  36.6 us
    ppermute x16, starting transfers between devices, extended(): lax.ppermute(head, axis, [((i + 1) % count, i) for i in range(ends)])  34.4 us
    psum x1, blocking collectives, axis_by_axis(): return lax.psum(partial, outer_axis)  31.1 us
    ppermute x16, starting transfers between devices, extended(): lax.ppermute(tail, axis, [(i, (i + 1) % count) for i in range(ends)])  27.2 us
    ppermute x16, waiting for transfers between devices, extended(): lax.ppermute(head, axis, [((i + 1) % count, i) for i in range(ends)])  15.6 us
    ppermute x16, waiting for transfers between devices, extended(): lax.ppermute(tail, axis, [(i, (i + 1) % count) for i in range(ends)])  11.9 us
    psum x1, blocking collectives, shards(): own_weight = lax.psum(spatial, 'dp')  9.03 us
  transfers between devices with their start and end apart: 33, of which 14 were waited for; matrix products, arithmetic and copies ran while one was open for 7% of the time, Pallas kernels for 0%

profile of v1, /device:TPU:0, one launch (start us, length us, event | category | flops | bytes accessed | tf_op | source)
XLA Modules:
  0.0 259.0 jit_solution(6203430556448238331)
XLA Ops:
  8.7 2.4 collective-permute-start
  15.0 36.6 %all-reduce.1 = (f32[1]{0:T(128)}, f32[1]{0:T(128)}) all-reduce(f32[1]{0:T(128)} %bitcast.2, f32[1]{0:T(128)} %bitcast.3), channel_id=1, replica_groups=mesh['dp'=2,'lat'=4,'lon'=4] {'lat','lon'}, use_global_device_ids=true, to_apply=%region_1.0 | all-reduce | flops 2 | bytes 16 | tf_op jit(solution)/shard_map/psum | solution.py:80
  56.2 1.5 fusion.171
  57.8 1.5 fusion.172
  61.0 3.7 %collective-permute-start.3 = (f32[2,18,1]{2,1,0:T(8,128)S(1)}, f32[2,18,1]{2,1,0:T(8,128)S(1)}, u32[]{:S(2)}, u32[]{:S(2)}) collective-permute-start(f32[2,18,1]{2,1,0:T(8,128)S(1)} %get-tuple-element.59), channel_id=1, source_target_pairs={{1,0},{2,1},{3,2},{0,3},{5,4},{6,5},{7,6},{4,7},{9,8},{10,9},{11,1... | collective-permute-start | bytes 440 | tf_op jit(solution)/shard_map/ppermute | solution.py:26
  64.7 2.0 collective-permute-start.7
  68.4 1.4 multiply_add_fusion.3
  69.8 2.6 %collective-permute-start.8 = (f32[1,1,128]{2,1,0:T(1,128)S(1)}, f32[1,1,128]{2,1,0:T(1,128)S(1)}, u32[]{:S(2)}, u32[]{:S(2)}) collective-permute-start(f32[1,1,128]{2,1,0:T(1,128)S(1)} %get-tuple-element.78), channel_id=1, source_target_pairs={{0,4},{4,8},{8,12},{1,5},{5,9},{9,13},{2,6},{6,10},{10,14},{3,7},{... | collective-permute-start | bytes 1544 | tf_op jit(solution)/shard_map/ppermute | solution.py:24
  73.8 4.7 %collective-permute-done.9 = f32[1,1,128]{2,1,0:T(1,128)S(1)} collective-permute-done((f32[1,1,128]{2,1,0:T(1,128)S(1)}, f32[1,1,128]{2,1,0:T(1,128)S(1)}, u32[]{:S(2)}, u32[]{:S(2)}) %collective-permute-start.9) | collective-permute-done | bytes 544 | tf_op jit(solution)/shard_map/ppermute | solution.py:26
  78.6 3.8 %collective-permute-start.11 = (f32[1,18,1]{2,1,0:T(8,128)S(1)}, f32[1,18,1]{2,1,0:T(8,128)S(1)}, u32[]{:S(2)}, u32[]{:S(2)}) collective-permute-start(f32[1,18,1]{2,1,0:T(8,128)S(1)} %get-tuple-element.69), channel_id=1, source_target_pairs={{1,0},{2,1},{3,2},{0,3},{5,4},{6,5},{7,6},{4,7},{9,8},{10,9},{11,1... | collective-permute-start | bytes 224 | tf_op jit(solution)/shard_map/ppermute | solution.py:26
  82.4 1.7 collective-permute-done.10
  85.3 3.3 %collective-permute-start.12 = (f32[1,1,128]{2,1,0:T(1,128)S(1)}, f32[1,1,128]{2,1,0:T(1,128)S(1)}, u32[]{:S(2)}, u32[]{:S(2)}) collective-permute-start(f32[1,1,128]{2,1,0:T(1,128)S(1)} %get-tuple-element.76), channel_id=1, source_target_pairs={{0,4},{4,8},{8,12},{1,5},{5,9},{9,13},{2,6},{6,10},{10,14},{3,7},{... | collective-permute-start | bytes 1544 | tf_op jit(solution)/shard_map/ppermute | solution.py:24
  90.0 2.2 collective-permute-done.13
  93.3 2.8 %collective-permute-start.15 = (f32[1,18,1]{2,1,0:T(8,128)S(1)}, f32[1,18,1]{2,1,0:T(8,128)S(1)}, u32[]{:S(2)}, u32[]{:S(2)}) collective-permute-start(f32[1,18,1]{2,1,0:T(8,128)S(1)} %get-tuple-element.67), channel_id=1, source_target_pairs={{1,0},{2,1},{3,2},{0,3},{5,4},{6,5},{7,6},{4,7},{9,8},{10,9},{11,1... | collective-permute-start | bytes 224 | tf_op jit(solution)/shard_map/ppermute | solution.py:26
  96.1 1.6 collective-permute-done.14
  99.1 3.4 %collective-permute-start.16 = (f32[1,1,128]{2,1,0:T(1,128)S(1)}, f32[1,1,128]{2,1,0:T(1,128)S(1)}, u32[]{:S(2)}, u32[]{:S(2)}) collective-permute-start(f32[1,1,128]{2,1,0:T(1,128)S(1)} %get-tuple-element.74), channel_id=1, source_target_pairs={{0,4},{4,8},{8,12},{1,5},{5,9},{9,13},{2,6},{6,10},{10,14},{3,7},{... | collective-permute-start | bytes 1544 | tf_op jit(solution)/shard_map/ppermute | solution.py:24
  103.8 2.2 collective-permute-done.17
  107.3 2.6 %collective-permute-start.19 = (f32[1,18,1]{2,1,0:T(8,128)S(1)}, f32[1,18,1]{2,1,0:T(8,128)S(1)}, u32[]{:S(2)}, u32[]{:S(2)}) collective-permute-start(f32[1,18,1]{2,1,0:T(8,128)S(1)} %get-tuple-element.65), channel_id=1, source_target_pairs={{1,0},{2,1},{3,2},{0,3},{5,4},{6,5},{7,6},{4,7},{9,8},{10,9},{11,1... | collective-permute-start | bytes 224 | tf_op jit(solution)/shard_map/ppermute | solution.py:26
  110.0 1.6 collective-permute-done.18
  113.0 3.4 %collective-permute-start.20 = (f32[1,1,128]{2,1,0:T(1,128)S(1)}, f32[1,1,128]{2,1,0:T(1,128)S(1)}, u32[]{:S(2)}, u32[]{:S(2)}) collective-permute-start(f32[1,1,128]{2,1,0:T(1,128)S(1)} %get-tuple-element.72), channel_id=1, source_target_pairs={{0,4},{4,8},{8,12},{1,5},{5,9},{9,13},{2,6},{6,10},{10,14},{3,7},{... | collective-permute-start | bytes 1544 | tf_op jit(solution)/shard_map/ppermute | solution.py:24
  117.7 3.5 %collective-permute-start.24 = (bf16[1,1,128,128]{3,2,1,0:T(8,128)(2,1)S(1)}, bf16[1,1,128,128]{3,2,1,0:T(8,128)(2,1)S(1)}, u32[]{:S(2)}, u32[]{:S(2)}) collective-permute-start(bf16[1,1,128,128]{3,2,1,0:T(8,128)(2,1)S(1)} %get-tuple-element.55), channel_id=1, source_target_pairs={{0,4},{4,8},{8,12},{1,5},{5,9},{9,13},{2,6},{6,10},{10,14},{3,7},{... | collective-permute-start | bytes 98312 | tf_op jit(solution)/shard_map/ppermute | solution.py:24
  123.9 2.6 %collective-permute-start.23 = (f32[1,18,1]{2,1,0:T(8,128)S(1)}, f32[1,18,1]{2,1,0:T(8,128)S(1)}, u32[]{:S(2)}, u32[]{:S(2)}) collective-permute-start(f32[1,18,1]{2,1,0:T(8,128)S(1)} %get-tuple-element.63), channel_id=1, source_target_pairs={{1,0},{2,1},{3,2},{0,3},{5,4},{6,5},{7,6},{4,7},{9,8},{10,9},{11,1... | collective-permute-start | bytes 224 | tf_op jit(solution)/shard_map/ppermute | solution.py:26
  126.5 1.6 collective-permute-done.22
  128.1 4.4 %fusion.69 = f32[2048]{0:T(1024)S(1)} fusion(f32[1,16,128]{2,1,0:T(8,128)S(1)} %get-tuple-element.14, f32[1,16,128]{2,1,0:T(8,128)S(1)} %get-tuple-element.24, f32[1,16,128]{2,1,0:T(8,128)S(1)} %get-tuple-element.13, f32[1,18,1]{2,1,0:T(8,128)S(1)} %collective-permute-done.23, f32[1,1,128]{2,1,0:T(1,128)S(1)} %collective-permute-done.21, ...), kind=kLoop, calls=%fused_computation.128 | loop fusion | flops 79872 | bytes 107692 | tf_op jit(solution)/shard_map/mul | solution.py:110
  134.3 2.6 %collective-permute-start.27 = (bf16[1,18,1,128]{3,2,1,0:T(2,128)(2,1)S(1)}, bf16[1,18,1,128]{3,2,1,0:T(2,128)(2,1)S(1)}, u32[]{:S(2)}, u32[]{:S(2)}) collective-permute-start(bf16[1,18,1,128]{3,2,1,0:T(2,128)(2,1)S(1)} %get-tuple-element.46), channel_id=1, source_target_pairs={{1,0},{2,1},{3,2},{0,3},{5,4},{6,5},{7,6},{4,7},{9,8},{10,9},{11,1... | collective-permute-start | bytes 13832 | tf_op jit(solution)/shard_map/ppermute | solution.py:26
  145.8 2.2 collective-permute-start.28
  150.5 3.9 %collective-permute-done.29 = bf16[1,1,128,128]{3,2,1,0:T(8,128)(2,1)S(1)} collective-permute-done((bf16[1,1,128,128]{3,2,1,0:T(8,128)(2,1)S(1)}, bf16[1,1,128,128]{3,2,1,0:T(8,128)(2,1)S(1)}, u32[]{:S(2)}, u32[]{:S(2)}) %collective-permute-start.29) | collective-permute-done | bytes 32800 | tf_op jit(solution)/shard_map/ppermute | solution.py:26
  154.4 3.9 %collective-permute-start.30 = (bf16[1,18,1,128]{3,2,1,0:T(2,128)(2,1)S(1)}, bf16[1,18,1,128]{3,2,1,0:T(2,128)(2,1)S(1)}, u32[]{:S(2)}, u32[]{:S(2)}) collective-permute-start(bf16[1,18,1,128]{3,2,1,0:T(2,128)(2,1)S(1)} %get-tuple-element.40), channel_id=1, source_target_pairs={{1,0},{2,1},{3,2},{0,3},{5,4},{6,5},{7,6},{4,7},{9,8},{10,9},{11,1... | collective-permute-start | bytes 13832 | tf_op jit(solution)/shard_map/ppermute | solution.py:26
  159.7 4.1 %collective-permute-done.31 = bf16[1,18,1,128]{3,2,1,0:T(2,128)(2,1)S(1)} collective-permute-done((bf16[1,18,1,128]{3,2,1,0:T(2,128)(2,1)S(1)}, bf16[1,18,1,128]{3,2,1,0:T(2,128)(2,1)S(1)}, u32[]{:S(2)}, u32[]{:S(2)}) %collective-permute-start.31) | collective-permute-done | bytes 4640 | tf_op jit(solution)/shard_map/ppermute | solution.py:24
  168.0 42.9 %reduce-scatter.2.cloned.1.call-done = f32[8,3,3,128]{3,0,2,1:T(8,128)} async-done(((f32[128,3,3,128]{3,0,2,1:T(8,128)}), f32[8,3,3,128]{3,0,2,1:T(8,128)}) %reduce-scatter.2.cloned.1.call-update) | async-done | bytes 36880 | tf_op jit(solution)/shard_map/reduce_scatter | solution.py:138
  210.8 9.0 %all-reduce.2 = (f32[8,3,3,128]{3,0,2,1:T(8,128)S(1)}, f32[128]{0:T(128)S(1)}, f32[128]{0:T(128)S(1)}) all-reduce(f32[8,3,3,128]{3,0,2,1:T(8,128)} %reduce-scatter.2.cloned.1.call-done, f32[128]{0:T(128)S(1)} %get-tuple-element.11, f32[128]{0:T(128)S(1)} %get-tuple-element.25), channel_id=1, replica_groups=mesh['dp'=2,'lat'=4,'lon'=4] {'dp'}, use_global_device_ids=true, to_apply=%region_5.0 | all-reduce | flops 9472 | bytes 75776 | tf_op jit(solution)/shard_map/psum | solution.py:144
  220.5 31.1 %all-reduce = (f32[128]{0:T(128)S(1)}, f32[128]{0:T(128)S(1)}) all-reduce(f32[128]{0:T(128)S(1)} %get-tuple-element.9, f32[128]{0:T(128)S(1)} %get-tuple-element.10), channel_id=1, replica_groups=mesh['dp'=2,'lat'=4,'lon'=4] {'lat','lon'}, use_global_device_ids=true, to_apply=%region_8.0 | all-reduce | flops 256 | bytes 2048 | tf_op jit(solution)/shard_map/psum | solution.py:13
  (121 shorter events, 46.2 us)
Async XLA Ops:
  7.2 203.7 %reduce-scatter.2.cloned.1.call-start = ((), (), s32[]{:S(2)}) async-start(), calls=%async_computation.1 | async-start | bytes 626688 | tf_op jit(solution)/shard_map/reduce_scatter | solution.py:138
  8.7 51.3 %collective-permute-start = (f32[2,1,128]{2,1,0:T(1,128)S(1)}, f32[2,1,128]{2,1,0:T(1,128)S(1)}, u32[]{:S(2)}, u32[]{:S(2)}) collective-permute-start(f32[2,1,128]{2,1,0:T(1,128)S(1)} %get-tuple-element.60), channel_id=1, source_target_pairs={{0,4},{4,8},{8,12},{1,5},{5,9},{9,13},{2,6},{6,10},{10,14},{3,7},{... | collective-permute-start | bytes 3080 | tf_op jit(solution)/shard_map/ppermute | solution.py:24
  11.1 49.0 %collective-permute-start.1 = (f32[2,1,128]{2,1,0:T(1,128)S(1)}, f32[2,1,128]{2,1,0:T(1,128)S(1)}, u32[]{:S(2)}, u32[]{:S(2)}) collective-permute-start(f32[2,1,128]{2,1,0:T(1,128)S(1)} %get-tuple-element.61), channel_id=1, source_target_pairs={{4,0},{8,4},{12,8},{5,1},{9,5},{13,9},{6,2},{10,6},{14,10},{7,3},{... | collective-permute-start | bytes 3080 | tf_op jit(solution)/shard_map/ppermute | solution.py:26
  53.6 5.6 %collective-permute-start.4 = (f32[1,1,128]{2,1,0:T(1,128)S(1)}, f32[1,1,128]{2,1,0:T(1,128)S(1)}, u32[]{:S(2)}, u32[]{:S(2)}) collective-permute-start(f32[1,1,128]{2,1,0:T(1,128)S(1)} %get-tuple-element.80), channel_id=1, source_target_pairs={{0,4},{4,8},{8,12},{1,5},{5,9},{9,13},{2,6},{6,10},{10,14},{3,7},{... | collective-permute-start | bytes 1544 | tf_op jit(solution)/shard_map/ppermute | solution.py:24
  54.9 5.0 %collective-permute-start.5 = (f32[1,1,128]{2,1,0:T(1,128)S(1)}, f32[1,1,128]{2,1,0:T(1,128)S(1)}, u32[]{:S(2)}, u32[]{:S(2)}) collective-permute-start(f32[1,1,128]{2,1,0:T(1,128)S(1)} %get-tuple-element.81), channel_id=1, source_target_pairs={{4,0},{8,4},{12,8},{5,1},{9,5},{13,9},{6,2},{10,6},{14,10},{7,3},{... | collective-permute-start | bytes 1544 | tf_op jit(solution)/shard_map/ppermute | solution.py:26
  60.0 7.5 %collective-permute-start.6 = (f32[1,18,1]{2,1,0:T(8,128)S(1)}, f32[1,18,1]{2,1,0:T(8,128)S(1)}, u32[]{:S(2)}, u32[]{:S(2)}) collective-permute-start(f32[1,18,1]{2,1,0:T(8,128)S(1)} %get-tuple-element.70), channel_id=1, source_target_pairs={{0,1},{1,2},{2,3},{3,0},{4,5},{5,6},{6,7},{7,4},{8,9},{9,10},{10,1... | collective-permute-start | bytes 224 | tf_op jit(solution)/shard_map/ppermute | solution.py:24
  60.8 5.8 %collective-permute-start.2 = (f32[2,18,1]{2,1,0:T(8,128)S(1)}, f32[2,18,1]{2,1,0:T(8,128)S(1)}, u32[]{:S(2)}, u32[]{:S(2)}) collective-permute-start(f32[2,18,1]{2,1,0:T(8,128)S(1)} %get-tuple-element.58), channel_id=1, source_target_pairs={{0,1},{1,2},{2,3},{3,0},{4,5},{5,6},{6,7},{7,4},{8,9},{9,10},{10,1... | collective-permute-start | bytes 440 | tf_op jit(solution)/shard_map/ppermute | solution.py:24
  61.0 5.7 %collective-permute-start.3 = (f32[2,18,1]{2,1,0:T(8,128)S(1)}, f32[2,18,1]{2,1,0:T(8,128)S(1)}, u32[]{:S(2)}, u32[]{:S(2)}) collective-permute-start(f32[2,18,1]{2,1,0:T(8,128)S(1)} %get-tuple-element.59), channel_id=1, source_target_pairs={{1,0},{2,1},{3,2},{0,3},{5,4},{6,5},{7,6},{4,7},{9,8},{10,9},{11,1... | collective-permute-start | bytes 440 | tf_op jit(solution)/shard_map/ppermute | solution.py:26
  64.7 3.7 %collective-permute-start.7 = (f32[1,18,1]{2,1,0:T(8,128)S(1)}, f32[1,18,1]{2,1,0:T(8,128)S(1)}, u32[]{:S(2)}, u32[]{:S(2)}) collective-permute-start(f32[1,18,1]{2,1,0:T(8,128)S(1)} %get-tuple-element.71), channel_id=1, source_target_pairs={{1,0},{2,1},{3,2},{0,3},{5,4},{6,5},{7,6},{4,7},{9,8},{10,9},{11,1... | collective-permute-start | bytes 224 | tf_op jit(solution)/shard_map/ppermute | solution.py:26
  69.8 3.9 %collective-permute-start.8 = (f32[1,1,128]{2,1,0:T(1,128)S(1)}, f32[1,1,128]{2,1,0:T(1,128)S(1)}, u32[]{:S(2)}, u32[]{:S(2)}) collective-permute-start(f32[1,1,128]{2,1,0:T(1,128)S(1)} %get-tuple-element.78), channel_id=1, source_target_pairs={{0,4},{4,8},{8,12},{1,5},{5,9},{9,13},{2,6},{6,10},{10,14},{3,7},{... | collective-permute-start | bytes 1544 | tf_op jit(solution)/shard_map/ppermute | solution.py:24
  72.4 6.0 %collective-permute-start.9 = (f32[1,1,128]{2,1,0:T(1,128)S(1)}, f32[1,1,128]{2,1,0:T(1,128)S(1)}, u32[]{:S(2)}, u32[]{:S(2)}) collective-permute-start(f32[1,1,128]{2,1,0:T(1,128)S(1)} %get-tuple-element.79), channel_id=1, source_target_pairs={{4,0},{8,4},{12,8},{5,1},{9,5},{13,9},{6,2},{10,6},{14,10},{7,3},{... | collective-permute-start | bytes 1544 | tf_op jit(solution)/shard_map/ppermute | solution.py:26
  78.5 5.5 %collective-permute-start.10 = (f32[1,18,1]{2,1,0:T(8,128)S(1)}, f32[1,18,1]{2,1,0:T(8,128)S(1)}, u32[]{:S(2)}, u32[]{:S(2)}) collective-permute-start(f32[1,18,1]{2,1,0:T(8,128)S(1)} %get-tuple-element.68), channel_id=1, source_target_pairs={{0,1},{1,2},{2,3},{3,0},{4,5},{5,6},{6,7},{7,4},{8,9},{9,10},{10,1... | collective-permute-start | bytes 224 | tf_op jit(solution)/shard_map/ppermute | solution.py:24
  78.6 5.5 %collective-permute-start.11 = (f32[1,18,1]{2,1,0:T(8,128)S(1)}, f32[1,18,1]{2,1,0:T(8,128)S(1)}, u32[]{:S(2)}, u32[]{:S(2)}) collective-permute-start(f32[1,18,1]{2,1,0:T(8,128)S(1)} %get-tuple-element.69), channel_id=1, source_target_pairs={{1,0},{2,1},{3,2},{0,3},{5,4},{6,5},{7,6},{4,7},{9,8},{10,9},{11,1... | collective-permute-start | bytes 224 | tf_op jit(solution)/shard_map/ppermute | solution.py:26
  85.3 4.6 %collective-permute-start.12 = (f32[1,1,128]{2,1,0:T(1,128)S(1)}, f32[1,1,128]{2,1,0:T(1,128)S(1)}, u32[]{:S(2)}, u32[]{:S(2)}) collective-permute-start(f32[1,1,128]{2,1,0:T(1,128)S(1)} %get-tuple-element.76), channel_id=1, source_target_pairs={{0,4},{4,8},{8,12},{1,5},{5,9},{9,13},{2,6},{6,10},{10,14},{3,7},{... | collective-permute-start | bytes 1544 | tf_op jit(solution)/shard_map/ppermute | solution.py:24
  88.7 3.5 %collective-permute-start.13 = (f32[1,1,128]{2,1,0:T(1,128)S(1)}, f32[1,1,128]{2,1,0:T(1,128)S(1)}, u32[]{:S(2)}, u32[]{:S(2)}) collective-permute-start(f32[1,1,128]{2,1,0:T(1,128)S(1)} %get-tuple-element.77), channel_id=1, source_target_pairs={{4,0},{8,4},{12,8},{5,1},{9,5},{13,9},{6,2},{10,6},{14,10},{7,3},{... | collective-permute-start | bytes 1544 | tf_op jit(solution)/shard_map/ppermute | solution.py:26
  92.3 5.5 %collective-permute-start.14 = (f32[1,18,1]{2,1,0:T(8,128)S(1)}, f32[1,18,1]{2,1,0:T(8,128)S(1)}, u32[]{:S(2)}, u32[]{:S(2)}) collective-permute-start(f32[1,18,1]{2,1,0:T(8,128)S(1)} %get-tuple-element.66), channel_id=1, source_target_pairs={{0,1},{1,2},{2,3},{3,0},{4,5},{5,6},{6,7},{7,4},{8,9},{9,10},{10,1... | collective-permute-start | bytes 224 | tf_op jit(solution)/shard_map/ppermute | solution.py:24
  93.3 4.4 %collective-permute-start.15 = (f32[1,18,1]{2,1,0:T(8,128)S(1)}, f32[1,18,1]{2,1,0:T(8,128)S(1)}, u32[]{:S(2)}, u32[]{:S(2)}) collective-permute-start(f32[1,18,1]{2,1,0:T(8,128)S(1)} %get-tuple-element.67), channel_id=1, source_target_pairs={{1,0},{2,1},{3,2},{0,3},{5,4},{6,5},{7,6},{4,7},{9,8},{10,9},{11,1... | collective-permute-start | bytes 224 | tf_op jit(solution)/shard_map/ppermute | solution.py:26
  99.1 4.7 %collective-permute-start.16 = (f32[1,1,128]{2,1,0:T(1,128)S(1)}, f32[1,1,128]{2,1,0:T(1,128)S(1)}, u32[]{:S(2)}, u32[]{:S(2)}) collective-permute-start(f32[1,1,128]{2,1,0:T(1,128)S(1)} %get-tuple-element.74), channel_id=1, source_target_pairs={{0,4},{4,8},{8,12},{1,5},{5,9},{9,13},{2,6},{6,10},{10,14},{3,7},{... | collective-permute-start | bytes 1544 | tf_op jit(solution)/shard_map/ppermute | solution.py:24
  106.1 5.5 %collective-permute-start.18 = (f32[1,18,1]{2,1,0:T(8,128)S(1)}, f32[1,18,1]{2,1,0:T(8,128)S(1)}, u32[]{:S(2)}, u32[]{:S(2)}) collective-permute-start(f32[1,18,1]{2,1,0:T(8,128)S(1)} %get-tuple-element.64), channel_id=1, source_target_pairs={{0,1},{1,2},{2,3},{3,0},{4,5},{5,6},{6,7},{7,4},{8,9},{9,10},{10,1... | collective-permute-start | bytes 224 | tf_op jit(solution)/shard_map/ppermute | solution.py:24
  107.3 4.2 %collective-permute-start.19 = (f32[1,18,1]{2,1,0:T(8,128)S(1)}, f32[1,18,1]{2,1,0:T(8,128)S(1)}, u32[]{:S(2)}, u32[]{:S(2)}) collective-permute-start(f32[1,18,1]{2,1,0:T(8,128)S(1)} %get-tuple-element.65), channel_id=1, source_target_pairs={{1,0},{2,1},{3,2},{0,3},{5,4},{6,5},{7,6},{4,7},{9,8},{10,9},{11,1... | collective-permute-start | bytes 224 | tf_op jit(solution)/shard_map/ppermute | solution.py:26
  113.0 9.5 %collective-permute-start.20 = (f32[1,1,128]{2,1,0:T(1,128)S(1)}, f32[1,1,128]{2,1,0:T(1,128)S(1)}, u32[]{:S(2)}, u32[]{:S(2)}) collective-permute-start(f32[1,1,128]{2,1,0:T(1,128)S(1)} %get-tuple-element.72), channel_id=1, source_target_pairs={{0,4},{4,8},{8,12},{1,5},{5,9},{9,13},{2,6},{6,10},{10,14},{3,7},{... | collective-permute-start | bytes 1544 | tf_op jit(solution)/shard_map/ppermute | solution.py:24
  116.4 6.1 %collective-permute-start.21 = (f32[1,1,128]{2,1,0:T(1,128)S(1)}, f32[1,1,128]{2,1,0:T(1,128)S(1)}, u32[]{:S(2)}, u32[]{:S(2)}) collective-permute-start(f32[1,1,128]{2,1,0:T(1,128)S(1)} %get-tuple-element.73), channel_id=1, source_target_pairs={{4,0},{8,4},{12,8},{5,1},{9,5},{13,9},{6,2},{10,6},{14,10},{7,3},{... | collective-permute-start | bytes 1544 | tf_op jit(solution)/shard_map/ppermute | solution.py:26
  117.7 14.9 %collective-permute-start.24 = (bf16[1,1,128,128]{3,2,1,0:T(8,128)(2,1)S(1)}, bf16[1,1,128,128]{3,2,1,0:T(8,128)(2,1)S(1)}, u32[]{:S(2)}, u32[]{:S(2)}) collective-permute-start(bf16[1,1,128,128]{3,2,1,0:T(8,128)(2,1)S(1)} %get-tuple-element.55), channel_id=1, source_target_pairs={{0,4},{4,8},{8,12},{1,5},{5,9},{9,13},{2,6},{6,10},{10,14},{3,7},{... | collective-permute-start | bytes 98312 | tf_op jit(solution)/shard_map/ppermute | solution.py:24
  121.2 11.4 %collective-permute-start.25 = (bf16[1,1,128,128]{3,2,1,0:T(8,128)(2,1)S(1)}, bf16[1,1,128,128]{3,2,1,0:T(8,128)(2,1)S(1)}, u32[]{:S(2)}, u32[]{:S(2)}) collective-permute-start(bf16[1,1,128,128]{3,2,1,0:T(8,128)(2,1)S(1)} %get-tuple-element.54), channel_id=1, source_target_pairs={{4,0},{8,4},{12,8},{5,1},{9,5},{13,9},{6,2},{10,6},{14,10},{7,3},{... | collective-permute-start | bytes 98312 | tf_op jit(solution)/shard_map/ppermute | solution.py:26
  122.6 5.5 %collective-permute-start.22 = (f32[1,18,1]{2,1,0:T(8,128)S(1)}, f32[1,18,1]{2,1,0:T(8,128)S(1)}, u32[]{:S(2)}, u32[]{:S(2)}) collective-permute-start(f32[1,18,1]{2,1,0:T(8,128)S(1)} %get-tuple-element.62), channel_id=1, source_target_pairs={{0,1},{1,2},{2,3},{3,0},{4,5},{5,6},{6,7},{7,4},{8,9},{9,10},{10,1... | collective-permute-start | bytes 224 | tf_op jit(solution)/shard_map/ppermute | solution.py:24
  123.9 4.2 %collective-permute-start.23 = (f32[1,18,1]{2,1,0:T(8,128)S(1)}, f32[1,18,1]{2,1,0:T(8,128)S(1)}, u32[]{:S(2)}, u32[]{:S(2)}) collective-permute-start(f32[1,18,1]{2,1,0:T(8,128)S(1)} %get-tuple-element.63), channel_id=1, source_target_pairs={{1,0},{2,1},{3,2},{0,3},{5,4},{6,5},{7,6},{4,7},{9,8},{10,9},{11,1... | collective-permute-start | bytes 224 | tf_op jit(solution)/shard_map/ppermute | solution.py:26
  133.0 5.6 %collective-permute-start.26 = (bf16[1,18,1,128]{3,2,1,0:T(2,128)(2,1)S(1)}, bf16[1,18,1,128]{3,2,1,0:T(2,128)(2,1)S(1)}, u32[]{:S(2)}, u32[]{:S(2)}) collective-permute-start(bf16[1,18,1,128]{3,2,1,0:T(2,128)(2,1)S(1)} %get-tuple-element.45), channel_id=1, source_target_pairs={{0,1},{1,2},{2,3},{3,0},{4,5},{5,6},{6,7},{7,4},{8,9},{9,10},{10,1... | collective-permute-start | bytes 13832 | tf_op jit(solution)/shard_map/ppermute | solution.py:24
  134.3 4.2 %collective-permute-start.27 = (bf16[1,18,1,128]{3,2,1,0:T(2,128)(2,1)S(1)}, bf16[1,18,1,128]{3,2,1,0:T(2,128)(2,1)S(1)}, u32[]{:S(2)}, u32[]{:S(2)}) collective-permute-start(bf16[1,18,1,128]{3,2,1,0:T(2,128)(2,1)S(1)} %get-tuple-element.46), channel_id=1, source_target_pairs={{1,0},{2,1},{3,2},{0,3},{5,4},{6,5},{7,6},{4,7},{9,8},{10,9},{11,1... | collective-permute-start | bytes 13832 | tf_op jit(solution)/shard_map/ppermute | solution.py:26
  145.8 4.7 %collective-permute-start.28 = (bf16[1,1,128,128]{3,2,1,0:T(8,128)(2,1)S(1)}, bf16[1,1,128,128]{3,2,1,0:T(8,128)(2,1)S(1)}, u32[]{:S(2)}, u32[]{:S(2)}) collective-permute-start(bf16[1,1,128,128]{3,2,1,0:T(8,128)(2,1)S(1)} %get-tuple-element.49), channel_id=1, source_target_pairs={{0,4},{4,8},{8,12},{1,5},{5,9},{9,13},{2,6},{6,10},{10,14},{3,7},{... | collective-permute-start | bytes 98312 | tf_op jit(solution)/shard_map/ppermute | solution.py:24
  148.0 6.4 %collective-permute-start.29 = (bf16[1,1,128,128]{3,2,1,0:T(8,128)(2,1)S(1)}, bf16[1,1,128,128]{3,2,1,0:T(8,128)(2,1)S(1)}, u32[]{:S(2)}, u32[]{:S(2)}) collective-permute-start(bf16[1,1,128,128]{3,2,1,0:T(8,128)(2,1)S(1)} %get-tuple-element.50), channel_id=1, source_target_pairs={{4,0},{8,4},{12,8},{5,1},{9,5},{13,9},{6,2},{10,6},{14,10},{7,3},{... | collective-permute-start | bytes 98312 | tf_op jit(solution)/shard_map/ppermute | solution.py:26
  154.4 5.3 %collective-permute-start.30 = (bf16[1,18,1,128]{3,2,1,0:T(2,128)(2,1)S(1)}, bf16[1,18,1,128]{3,2,1,0:T(2,128)(2,1)S(1)}, u32[]{:S(2)}, u32[]{:S(2)}) collective-permute-start(bf16[1,18,1,128]{3,2,1,0:T(2,128)(2,1)S(1)} %get-tuple-element.40), channel_id=1, source_target_pairs={{1,0},{2,1},{3,2},{0,3},{5,4},{6,5},{7,6},{4,7},{9,8},{10,9},{11,1... | collective-permute-start | bytes 13832 | tf_op jit(solution)/shard_map/ppermute | solution.py:26
  158.3 5.5 %collective-permute-start.31 = (bf16[1,18,1,128]{3,2,1,0:T(2,128)(2,1)S(1)}, bf16[1,18,1,128]{3,2,1,0:T(2,128)(2,1)S(1)}, u32[]{:S(2)}, u32[]{:S(2)}) collective-permute-start(bf16[1,18,1,128]{3,2,1,0:T(2,128)(2,1)S(1)} %get-tuple-element.41), channel_id=1, source_target_pairs={{0,1},{1,2},{2,3},{3,0},{4,5},{5,6},{6,7},{7,4},{8,9},{9,10},{10,1... | collective-permute-start | bytes 13832 | tf_op jit(solution)/shard_map/ppermute | solution.py:24
  (7 other events, 241.5 us)
Sparse Core Ops, SparseCore 0:
  150.7 60.1 reduce-scatter.1
